TPU v7x, 32 devices: a whole 2x2x4 slice. The times are simulated.
32 devices in a mesh: dp: 8 (over y, x, core), tensor: 4 (over z).
Axes of the slice: x: 2, y: 2, z: 4, core: 2. Of those that a mesh axis runs over, the one named last changes fastest.
Arguments:
- img_hidden: bfloat16 [4096, 4304], P('dp', 'tensor'), may hold values from -0.25 to 0.25
- img_down: bfloat16 [4304, 1152], P('tensor'), may hold values from -0.09375 to 0.09375
- img_pooled: bfloat16 [4096, 1152], P(('dp', 'tensor')), may hold values from -0.25 to 0.25
- txt_hidden: bfloat16 [4096, 1152], P('dp', 'tensor'), may hold values from -0.25 to 0.25
- txt_proj: bfloat16 [1152, 1152], P('tensor'), may hold values from -0.1875 to 0.1875
- log_temp: float32 [1], replicated, may hold values from 1 to 2
- bias: float32 [1], replicated, may hold values from -4 to -1
- match: int32 [4096], P(('dp', 'tensor')), may hold values from 0 to 4095
- window_index: int32 [1], replicated, may hold values from 0 to 1
Outputs:
- img_grad: float32 [4096, 1152], P(('dp', 'tensor'))
- txt_grad: float32 [4096, 1152], P(('dp', 'tensor'))
- row_loss: float32 [4096], P(('dp', 'tensor'))
All inputs are finite; a program needn't handle non-finite values.
Results may differ from a plain program's by a relative error of at most 0.0039.
Values may be sent and summed in bfloat16 or wider, within the bound.
A program may use at most 64 MiB of HBM per device.

v0:
```python
import jax
import jax.numpy as jnp
from jax import lax
from jax.sharding import PartitionSpec as P

STEPS = 16


def shifted(shard, axis, by):
    devices = lax.axis_size(axis)
    return lax.ppermute(shard, axis, [(i, (i + by) % devices) for i in range(devices)])


def unit_rows(emb):
    length = jnp.sqrt(jnp.sum(emb * emb, axis=1, keepdims=True) + 1e-06)
    return (emb / length, length)


def pair_tile(image_low, text_block, owner, match, scale, shift_value):
    cosine = lax.dot_general(
        image_low, text_block, (((1,), (1,)), ((), ())), preferred_element_type=jnp.float32
    )
    text_index = owner * text_block.shape[0] + lax.iota(jnp.int32, text_block.shape[0])
    positive = match[:, None] == text_index[None, :]
    logit = scale * cosine + shift_value
    pair_loss = jnp.sum(
        jnp.where(positive, jax.nn.softplus(-logit), jax.nn.softplus(logit)), axis=1
    )
    coef = ((jax.nn.sigmoid(logit) - positive.astype(jnp.float32)) * scale).astype(jnp.bfloat16)
    image_part = jnp.dot(coef, text_block, preferred_element_type=jnp.float32)
    text_part = lax.dot_general(
        coef, image_low, (((0,), (0,)), ((), ())), preferred_element_type=jnp.float32
    )
    return (pair_loss, image_part, text_part)


def offset_blocks(blocks, window):
    windows = lax.axis_size(("dp", "tensor")) // STEPS
    for level in range((windows - 1).bit_length()):
        moved = shifted(blocks, ("dp", "tensor"), STEPS << level)
        blocks = jnp.where(window >> level & 1 == 1, moved, blocks)
    return blocks


def return_home(text_sum, fixed_steps, window):
    text_sum = shifted(text_sum, ("dp", "tensor"), -fixed_steps)
    windows = lax.axis_size(("dp", "tensor")) // STEPS
    for level in range((windows - 1).bit_length()):
        moved = shifted(text_sum, ("dp", "tensor"), -(STEPS << level))
        text_sum = jnp.where(window >> level & 1 == 1, moved, text_sum)
    return text_sum


def body(
    img_hidden, img_down, img_pooled, txt_hidden, txt_proj, log_temp, bias, match, window_index
):
    width = img_pooled.shape[1]
    summed = lax.psum_scatter(
        jnp.concatenate(
            [
                jnp.dot(img_hidden, img_down, preferred_element_type=jnp.float32),
                jnp.dot(txt_hidden, txt_proj, preferred_element_type=jnp.float32),
            ],
            axis=1,
        ),
        "tensor",
        scatter_dimension=0,
        tiled=True,
    )
    img_emb = summed[:, :width] + img_pooled.astype(jnp.float32)
    txt_emb = summed[:, width:]
    img_unit, img_len = unit_rows(img_emb)
    txt_unit, txt_len = unit_rows(txt_emb)
    image_low = img_unit.astype(jnp.bfloat16)
    text_low = txt_unit.astype(jnp.bfloat16)
    scale = jnp.exp(log_temp[0])
    shift_value = bias[0]
    window = window_index[0]
    start_step = window * STEPS
    position = lax.axis_index(("dp", "tensor"))
    devices = lax.axis_size(("dp", "tensor"))
    half_steps = STEPS // 2
    late_copy = shifted(text_low, ("dp", "tensor"), STEPS - 1)
    stacked = offset_blocks(jnp.stack([text_low, late_copy]), window)
    early_block = stacked[0]
    late_block = stacked[1]
    early_owner = (position - start_step) % devices
    late_owner = (position - start_step - (STEPS - 1)) % devices
    early_loss, early_image, early_sum = pair_tile(
        image_low, early_block, early_owner, match, scale, shift_value
    )
    late_loss, late_image, late_sum = pair_tile(
        image_low, late_block, late_owner, match, scale, shift_value
    )

    def two_turn(turn, carry):
        early_now, late_now, early_acc, late_acc, image_now, loss_now = carry
        early_now = shifted(early_now, ("dp", "tensor"), 1)
        late_now = shifted(late_now, ("dp", "tensor"), -1)
        early_acc = shifted(early_acc, ("dp", "tensor"), 1)
        late_acc = shifted(late_acc, ("dp", "tensor"), -1)
        owner_early = (position - start_step - turn) % devices
        owner_late = (position - start_step - (STEPS - 1) + turn) % devices
        loss_one, image_one, text_one = pair_tile(
            image_low, early_now, owner_early, match, scale, shift_value
        )
        loss_two, image_two, text_two = pair_tile(
            image_low, late_now, owner_late, match, scale, shift_value
        )
        return (
            early_now,
            late_now,
            early_acc + text_one,
            late_acc + text_two,
            image_now + image_one + image_two,
            loss_now + loss_one + loss_two,
        )

    carried = lax.fori_loop(
        1,
        half_steps,
        two_turn,
        (
            early_block,
            late_block,
            early_sum,
            late_sum,
            early_image + late_image,
            early_loss + late_loss,
        ),
    )
    early_sum = carried[2]
    late_sum = carried[3]
    image_dunit = carried[4]
    row_loss = carried[5]
    late_moved = shifted(late_sum, ("dp", "tensor"), -1)
    text_dunit = return_home(early_sum + late_moved, half_steps - 1, window)
    img_grad = (
        image_dunit - img_unit * jnp.sum(img_unit * image_dunit, axis=1, keepdims=True)
    ) / img_len
    txt_grad = (
        text_dunit - txt_unit * jnp.sum(txt_unit * text_dunit, axis=1, keepdims=True)
    ) / txt_len
    return (img_grad, txt_grad, row_loss)


def solution(mesh):
    in_specs = (
        P("dp", "tensor"),
        P("tensor", None),
        P(("dp", "tensor"), None),
        P("dp", "tensor"),
        P("tensor", None),
        P(),
        P(),
        P(("dp", "tensor")),
        P(),
    )
    out_specs = (P(("dp", "tensor"), None), P(("dp", "tensor"), None), P(("dp", "tensor")))
    return jax.shard_map(body, mesh=mesh, in_specs=in_specs, out_specs=out_specs, check_vma=False)
```

profile of v0, /device:TPU:0, one launch (start us, length us, event | category | flops | bytes accessed | tf_op | source)
XLA Modules:
  0.0 501.8 jit_solution(10158499696137616305)
XLA Ops:
  8.9 3.1 fusion.44
  12.9 2.5 pad_maximum_fusion
  15.4 88.2 %reduce-scatter.2.cloned.1.call-done = f32[128,2304]{1,0:T(8,128)} async-done(((f32[512,2304]{1,0:T(8,128)}), f32[128,2304]{1,0:T(8,128)}) %reduce-scatter.2.cloned.1.call-update) | async-done | bytes 1179664 | tf_op jit(solution)/shard_map/reduce_scatter | solution.py:58
  106.4 3.1 collective-permute-start.4
  109.6 7.4 %collective-permute-done.4 = bf16[128,1152]{1,0:T(8,128)(2,1)S(1)} collective-permute-done((bf16[128,1152]{1,0:T(8,128)(2,1)S(1)}, bf16[128,1152]{1,0:T(8,128)(2,1)S(1)}, u32[]{:S(2)}, u32[]{:S(2)}) %collective-permute-start.4) | collective-permute-done | bytes 294944 | tf_op jit(solution)/shard_map/ppermute | solution.py:11
  120.5 13.1 %collective-permute-done.5 = bf16[2,128,1152]{2,1,0:T(8,128)(2,1)} collective-permute-done((bf16[2,128,1152]{2,1,0:T(8,128)(2,1)}, bf16[2,128,1152]{2,1,0:T(8,128)(2,1)}, u32[]{:S(2)}, u32[]{:S(2)}) %collective-permute-start.5) | collective-permute-done | bytes 589856 | tf_op jit(solution)/shard_map/ppermute | solution.py:11
  139.9 303.8 %while.25 = (s32[]{:T(128)}, bf16[128,1152]{1,0:T(8,128)(2,1)}, bf16[128,1152]{1,0:T(8,128)(2,1)}, f32[128,1152]{1,0:T(8,128)}, f32[128,1152]{1,0:T(8,128)}, /*i...) while((s32[]{:T(128)}, bf16[128,1152]{1,0:T(8,128)(2,1)}, ...), condition=%wide.region_8.9_spmd, body=%wide.region_5.8_spmd.sunk | while | flops 228196640 | bytes 20523184 | solution.py:119
  139.9 2.9 collective-permute-start.1
  142.9 5.4 %collective-permute-start.3 = (f32[128,1152]{1,0:T(8,128)}, f32[128,1152]{1,0:T(8,128)}, u32[]{:S(2)}, u32[]{:S(2)}) collective-permute-start(f32[128,1152]{1,0:T(8,128)} %get-tuple-element.483), channel_id=1, source_target_pairs={{0,31},{1,0},{2,1},{3,2},{4,3},{5,4},{6,5},{7,6},{8,7},{9,8},{10,9... | collective-permute-start | bytes 1769480 | tf_op jit(solution)/shard_map/while/body/eval_jaxpr/ppermute | solution.py:11
  150.9 5.2 %collective-permute-done = bf16[128,1152]{1,0:T(8,128)(2,1)S(1)} collective-permute-done((bf16[128,1152]{1,0:T(8,128)(2,1)}, bf16[128,1152]{1,0:T(8,128)(2,1)S(1)}, u32[]{:S(2)}, u32[]{:S(2)}) %collective-permute-start) | collective-permute-done | bytes 294944 | tf_op jit(solution)/shard_map/while/body/eval_jaxpr/ppermute | solution.py:11
  158.9 9.9 %collective-permute-done.2 = f32[128,1152]{1,0:T(8,128)} collective-permute-done((f32[128,1152]{1,0:T(8,128)}, f32[128,1152]{1,0:T(8,128)}, u32[]{:S(2)}, u32[]{:S(2)}) %collective-permute-start.2) | collective-permute-done | bytes 589856 | tf_op jit(solution)/shard_map/while/body/eval_jaxpr/ppermute | solution.py:11
  168.8 2.2 convolution_add_fusion.6
  171.0 10.3 %collective-permute-done.3 = f32[128,1152]{1,0:T(8,128)} collective-permute-done((f32[128,1152]{1,0:T(8,128)}, f32[128,1152]{1,0:T(8,128)}, u32[]{:S(2)}, u32[]{:S(2)}) %collective-permute-start.3) | collective-permute-done | bytes 589856 | tf_op jit(solution)/shard_map/while/body/eval_jaxpr/ppermute | solution.py:11
  181.3 2.2 convolution_add_fusion.7
  183.4 5.5 %collective-permute-start.1 = (bf16[128,1152]{1,0:T(8,128)(2,1)}, bf16[128,1152]{1,0:T(8,128)(2,1)S(1)}, u32[]{:S(2)}, u32[]{:S(2)}) collective-permute-start(bf16[128,1152]{1,0:T(8,128)(2,1)} %get-tuple-element.481), channel_id=1, source_target_pairs={{0,31},{1,0},{2,1},{3,2},{4,3},{5,4},{6,5},{7,6},{8,7},{9,8},{10,9... | collective-permute-start | bytes 884744 | tf_op jit(solution)/shard_map/while/body/eval_jaxpr/ppermute | solution.py:11
  188.9 5.4 %collective-permute-start.3 = (f32[128,1152]{1,0:T(8,128)}, f32[128,1152]{1,0:T(8,128)}, u32[]{:S(2)}, u32[]{:S(2)}) collective-permute-start(f32[128,1152]{1,0:T(8,128)} %get-tuple-element.483), channel_id=1, source_target_pairs={{0,31},{1,0},{2,1},{3,2},{4,3},{5,4},{6,5},{7,6},{8,7},{9,8},{10,9... | collective-permute-start | bytes 1769480 | tf_op jit(solution)/shard_map/while/body/eval_jaxpr/ppermute | solution.py:11
  194.3 2.4 collective-permute-done.1
  197.9 5.2 %collective-permute-done = bf16[128,1152]{1,0:T(8,128)(2,1)S(1)} collective-permute-done((bf16[128,1152]{1,0:T(8,128)(2,1)}, bf16[128,1152]{1,0:T(8,128)(2,1)S(1)}, u32[]{:S(2)}, u32[]{:S(2)}) %collective-permute-start) | collective-permute-done | bytes 294944 | tf_op jit(solution)/shard_map/while/body/eval_jaxpr/ppermute | solution.py:11
  205.9 9.9 %collective-permute-done.2 = f32[128,1152]{1,0:T(8,128)} collective-permute-done((f32[128,1152]{1,0:T(8,128)}, f32[128,1152]{1,0:T(8,128)}, u32[]{:S(2)}, u32[]{:S(2)}) %collective-permute-start.2) | collective-permute-done | bytes 589856 | tf_op jit(solution)/shard_map/while/body/eval_jaxpr/ppermute | solution.py:11
  215.8 2.2 convolution_add_fusion.6
  218.0 9.5 %collective-permute-done.3 = f32[128,1152]{1,0:T(8,128)} collective-permute-done((f32[128,1152]{1,0:T(8,128)}, f32[128,1152]{1,0:T(8,128)}, u32[]{:S(2)}, u32[]{:S(2)}) %collective-permute-start.3) | collective-permute-done | bytes 589856 | tf_op jit(solution)/shard_map/while/body/eval_jaxpr/ppermute | solution.py:11
  227.5 2.2 convolution_add_fusion.7
  229.6 5.5 %collective-permute-start.1 = (bf16[128,1152]{1,0:T(8,128)(2,1)}, bf16[128,1152]{1,0:T(8,128)(2,1)S(1)}, u32[]{:S(2)}, u32[]{:S(2)}) collective-permute-start(bf16[128,1152]{1,0:T(8,128)(2,1)} %get-tuple-element.481), channel_id=1, source_target_pairs={{0,31},{1,0},{2,1},{3,2},{4,3},{5,4},{6,5},{7,6},{8,7},{9,8},{10,9... | collective-permute-start | bytes 884744 | tf_op jit(solution)/shard_map/while/body/eval_jaxpr/ppermute | solution.py:11
  235.1 5.4 %collective-permute-start.3 = (f32[128,1152]{1,0:T(8,128)}, f32[128,1152]{1,0:T(8,128)}, u32[]{:S(2)}, u32[]{:S(2)}) collective-permute-start(f32[128,1152]{1,0:T(8,128)} %get-tuple-element.483), channel_id=1, source_target_pairs={{0,31},{1,0},{2,1},{3,2},{4,3},{5,4},{6,5},{7,6},{8,7},{9,8},{10,9... | collective-permute-start | bytes 1769480 | tf_op jit(solution)/shard_map/while/body/eval_jaxpr/ppermute | solution.py:11
  240.5 2.3 collective-permute-done.1
  244.1 5.3 %collective-permute-done = bf16[128,1152]{1,0:T(8,128)(2,1)S(1)} collective-permute-done((bf16[128,1152]{1,0:T(8,128)(2,1)}, bf16[128,1152]{1,0:T(8,128)(2,1)S(1)}, u32[]{:S(2)}, u32[]{:S(2)}) %collective-permute-start) | collective-permute-done | bytes 294944 | tf_op jit(solution)/shard_map/while/body/eval_jaxpr/ppermute | solution.py:11
  252.1 9.9 %collective-permute-done.2 = f32[128,1152]{1,0:T(8,128)} collective-permute-done((f32[128,1152]{1,0:T(8,128)}, f32[128,1152]{1,0:T(8,128)}, u32[]{:S(2)}, u32[]{:S(2)}) %collective-permute-start.2) | collective-permute-done | bytes 589856 | tf_op jit(solution)/shard_map/while/body/eval_jaxpr/ppermute | solution.py:11
  262.0 2.2 convolution_add_fusion.6
  264.2 7.7 %collective-permute-done.3 = f32[128,1152]{1,0:T(8,128)} collective-permute-done((f32[128,1152]{1,0:T(8,128)}, f32[128,1152]{1,0:T(8,128)}, u32[]{:S(2)}, u32[]{:S(2)}) %collective-permute-start.3) | collective-permute-done | bytes 589856 | tf_op jit(solution)/shard_map/while/body/eval_jaxpr/ppermute | solution.py:11
  271.8 2.2 convolution_add_fusion.7
  274.0 5.5 %collective-permute-start.1 = (bf16[128,1152]{1,0:T(8,128)(2,1)}, bf16[128,1152]{1,0:T(8,128)(2,1)S(1)}, u32[]{:S(2)}, u32[]{:S(2)}) collective-permute-start(bf16[128,1152]{1,0:T(8,128)(2,1)} %get-tuple-element.481), channel_id=1, source_target_pairs={{0,31},{1,0},{2,1},{3,2},{4,3},{5,4},{6,5},{7,6},{8,7},{9,8},{10,9... | collective-permute-start | bytes 884744 | tf_op jit(solution)/shard_map/while/body/eval_jaxpr/ppermute | solution.py:11
  279.5 5.4 %collective-permute-start.3 = (f32[128,1152]{1,0:T(8,128)}, f32[128,1152]{1,0:T(8,128)}, u32[]{:S(2)}, u32[]{:S(2)}) collective-permute-start(f32[128,1152]{1,0:T(8,128)} %get-tuple-element.483), channel_id=1, source_target_pairs={{0,31},{1,0},{2,1},{3,2},{4,3},{5,4},{6,5},{7,6},{8,7},{9,8},{10,9... | collective-permute-start | bytes 1769480 | tf_op jit(solution)/shard_map/while/body/eval_jaxpr/ppermute | solution.py:11
  284.9 2.3 collective-permute-done.1
  288.4 5.2 %collective-permute-done = bf16[128,1152]{1,0:T(8,128)(2,1)S(1)} collective-permute-done((bf16[128,1152]{1,0:T(8,128)(2,1)}, bf16[128,1152]{1,0:T(8,128)(2,1)S(1)}, u32[]{:S(2)}, u32[]{:S(2)}) %collective-permute-start) | collective-permute-done | bytes 294944 | tf_op jit(solution)/shard_map/while/body/eval_jaxpr/ppermute | solution.py:11
  296.4 9.9 %collective-permute-done.2 = f32[128,1152]{1,0:T(8,128)} collective-permute-done((f32[128,1152]{1,0:T(8,128)}, f32[128,1152]{1,0:T(8,128)}, u32[]{:S(2)}, u32[]{:S(2)}) %collective-permute-start.2) | collective-permute-done | bytes 589856 | tf_op jit(solution)/shard_map/while/body/eval_jaxpr/ppermute | solution.py:11
  306.3 2.2 convolution_add_fusion.6
  308.5 6.0 %collective-permute-done.3 = f32[128,1152]{1,0:T(8,128)} collective-permute-done((f32[128,1152]{1,0:T(8,128)}, f32[128,1152]{1,0:T(8,128)}, u32[]{:S(2)}, u32[]{:S(2)}) %collective-permute-start.3) | collective-permute-done | bytes 589856 | tf_op jit(solution)/shard_map/while/body/eval_jaxpr/ppermute | solution.py:11
  316.6 5.5 %collective-permute-start.1 = (bf16[128,1152]{1,0:T(8,128)(2,1)}, bf16[128,1152]{1,0:T(8,128)(2,1)S(1)}, u32[]{:S(2)}, u32[]{:S(2)}) collective-permute-start(bf16[128,1152]{1,0:T(8,128)(2,1)} %get-tuple-element.481), channel_id=1, source_target_pairs={{0,31},{1,0},{2,1},{3,2},{4,3},{5,4},{6,5},{7,6},{8,7},{9,8},{10,9... | collective-permute-start | bytes 884744 | tf_op jit(solution)/shard_map/while/body/eval_jaxpr/ppermute | solution.py:11
  322.1 5.4 %collective-permute-start.3 = (f32[128,1152]{1,0:T(8,128)}, f32[128,1152]{1,0:T(8,128)}, u32[]{:S(2)}, u32[]{:S(2)}) collective-permute-start(f32[128,1152]{1,0:T(8,128)} %get-tuple-element.483), channel_id=1, source_target_pairs={{0,31},{1,0},{2,1},{3,2},{4,3},{5,4},{6,5},{7,6},{8,7},{9,8},{10,9... | collective-permute-start | bytes 1769480 | tf_op jit(solution)/shard_map/while/body/eval_jaxpr/ppermute | solution.py:11
  327.5 2.3 collective-permute-done.1
  331.1 5.1 %collective-permute-done = bf16[128,1152]{1,0:T(8,128)(2,1)S(1)} collective-permute-done((bf16[128,1152]{1,0:T(8,128)(2,1)}, bf16[128,1152]{1,0:T(8,128)(2,1)S(1)}, u32[]{:S(2)}, u32[]{:S(2)}) %collective-permute-start) | collective-permute-done | bytes 294944 | tf_op jit(solution)/shard_map/while/body/eval_jaxpr/ppermute | solution.py:11
  339.0 9.8 %collective-permute-done.2 = f32[128,1152]{1,0:T(8,128)} collective-permute-done((f32[128,1152]{1,0:T(8,128)}, f32[128,1152]{1,0:T(8,128)}, u32[]{:S(2)}, u32[]{:S(2)}) %collective-permute-start.2) | collective-permute-done | bytes 589856 | tf_op jit(solution)/shard_map/while/body/eval_jaxpr/ppermute | solution.py:11
  348.8 2.2 convolution_add_fusion.6
  351.0 5.0 collective-permute-done.3
  356.0 2.2 convolution_add_fusion.7
  358.1 4.9 collective-permute-start.1
  363.0 5.4 %collective-permute-start.3 = (f32[128,1152]{1,0:T(8,128)}, f32[128,1152]{1,0:T(8,128)}, u32[]{:S(2)}, u32[]{:S(2)}) collective-permute-start(f32[128,1152]{1,0:T(8,128)} %get-tuple-element.483), channel_id=1, source_target_pairs={{0,31},{1,0},{2,1},{3,2},{4,3},{5,4},{6,5},{7,6},{8,7},{9,8},{10,9... | collective-permute-start | bytes 1769480 | tf_op jit(solution)/shard_map/while/body/eval_jaxpr/ppermute | solution.py:11
  368.4 2.3 collective-permute-done.1
  371.9 5.2 %collective-permute-done = bf16[128,1152]{1,0:T(8,128)(2,1)S(1)} collective-permute-done((bf16[128,1152]{1,0:T(8,128)(2,1)}, bf16[128,1152]{1,0:T(8,128)(2,1)S(1)}, u32[]{:S(2)}, u32[]{:S(2)}) %collective-permute-start) | collective-permute-done | bytes 294944 | tf_op jit(solution)/shard_map/while/body/eval_jaxpr/ppermute | solution.py:11
  379.9 9.9 %collective-permute-done.2 = f32[128,1152]{1,0:T(8,128)} collective-permute-done((f32[128,1152]{1,0:T(8,128)}, f32[128,1152]{1,0:T(8,128)}, u32[]{:S(2)}, u32[]{:S(2)}) %collective-permute-start.2) | collective-permute-done | bytes 589856 | tf_op jit(solution)/shard_map/while/body/eval_jaxpr/ppermute | solution.py:11
  389.8 2.2 convolution_add_fusion.6
  392.0 7.2 %collective-permute-done.3 = f32[128,1152]{1,0:T(8,128)} collective-permute-done((f32[128,1152]{1,0:T(8,128)}, f32[128,1152]{1,0:T(8,128)}, u32[]{:S(2)}, u32[]{:S(2)}) %collective-permute-start.3) | collective-permute-done | bytes 589856 | tf_op jit(solution)/shard_map/while/body/eval_jaxpr/ppermute | solution.py:11
  399.2 2.2 convolution_add_fusion.7
  405.2 3.7 collective-permute-start.3
  408.9 3.1 collective-permute-done.1
  413.2 4.5 collective-permute-done
  420.6 9.9 %collective-permute-done.2 = f32[128,1152]{1,0:T(8,128)} collective-permute-done((f32[128,1152]{1,0:T(8,128)}, f32[128,1152]{1,0:T(8,128)}, u32[]{:S(2)}, u32[]{:S(2)}) %collective-permute-start.2) | collective-permute-done | bytes 589856 | tf_op jit(solution)/shard_map/while/body/eval_jaxpr/ppermute | solution.py:11
  430.4 2.2 convolution_add_fusion.6
  432.6 9.0 %collective-permute-done.3 = f32[128,1152]{1,0:T(8,128)} collective-permute-done((f32[128,1152]{1,0:T(8,128)}, f32[128,1152]{1,0:T(8,128)}, u32[]{:S(2)}, u32[]{:S(2)}) %collective-permute-start.3) | collective-permute-done | bytes 589856 | tf_op jit(solution)/shard_map/while/body/eval_jaxpr/ppermute | solution.py:11
  441.6 2.2 convolution_add_fusion.7
  443.8 3.4 collective-permute-start.6
  447.2 11.9 %collective-permute-done.6 = f32[128,1152]{1,0:T(8,128)S(1)} collective-permute-done((f32[128,1152]{1,0:T(8,128)}, f32[128,1152]{1,0:T(8,128)S(1)}, u32[]{:S(2)}, u32[]{:S(2)}) %collective-permute-start.6) | collective-permute-done | bytes 589856 | tf_op jit(solution)/shard_map/ppermute | solution.py:11
  460.3 15.7 %collective-permute-done.7 = f32[128,1152]{1,0:T(8,128)S(1)} collective-permute-done((f32[128,1152]{1,0:T(8,128)S(1)}, f32[128,1152]{1,0:T(8,128)S(1)}, u32[]{:S(2)}, u32[]{:S(2)}) %collective-permute-start.7) | collective-permute-done | bytes 589856 | tf_op jit(solution)/shard_map/ppermute | solution.py:11
  476.0 16.1 %collective-permute-done.8 = f32[128,1152]{1,0:T(8,128)S(1)} collective-permute-done((f32[128,1152]{1,0:T(8,128)S(1)}, f32[128,1152]{1,0:T(8,128)S(1)}, u32[]{:S(2)}, u32[]{:S(2)}) %collective-permute-start.8) | collective-permute-done | bytes 589856 | tf_op jit(solution)/shard_map/ppermute | solution.py:11
  (142 shorter events, 52.8 us)
Async XLA Ops:
  7.2 1.7 copy-start
  7.2 4.8 copy-start.9
  7.2 4.8 copy-start.7
  7.2 96.4 %reduce-scatter.2.cloned.1.call-start = ((), (), s32[]{:S(2)}) async-start(), calls=%async_computation.1 | async-start | bytes 5898240 | tf_op jit(solution)/shard_map/reduce_scatter | solution.py:58
  15.4 88.2 %copy-start.5 = (bf16[128,1152]{1,0:T(8,128)(2,1)S(1)}, bf16[128,1152]{1,0:T(8,128)(2,1)}, u32[]{:S(2)}) copy-start(bf16[128,1152]{1,0:T(8,128)(2,1)} %param.13) | copy-start | bytes 884740
  106.4 28.5 %copy-start.8 = (s32[128]{0:T(128)S(1)}, s32[128]{0:T(128)}, u32[]{:S(2)}) copy-start(s32[128]{0:T(128)} %param.18) | copy-start | bytes 1540
  106.4 10.5 %collective-permute-start.4 = (bf16[128,1152]{1,0:T(8,128)(2,1)S(1)}, bf16[128,1152]{1,0:T(8,128)(2,1)S(1)}, u32[]{:S(2)}, u32[]{:S(2)}) collective-permute-start(bf16[128,1152]{1,0:T(8,128)(2,1)S(1)} %get-tuple-element.364), channel_id=1, source_target_pairs={{0,15},{1,16},{2,17},{3,18},{4,19},{5,20},{6,21},{7,22},{8,23},{9,... | collective-permute-start | bytes 884744 | tf_op jit(solution)/shard_map/ppermute | solution.py:11
  117.8 15.7 %collective-permute-start.5 = (bf16[2,128,1152]{2,1,0:T(8,128)(2,1)}, bf16[2,128,1152]{2,1,0:T(8,128)(2,1)}, u32[]{:S(2)}, u32[]{:S(2)}) collective-permute-start(bf16[2,128,1152]{2,1,0:T(8,128)(2,1)} %pad_maximum_fusion.1), channel_id=1, source_target_pairs={{0,16},{1,17},{2,18},{3,19},{4,20},{5,21},{6,22},{7,23},{8,24},{9,... | collective-permute-start | bytes 1769480 | tf_op jit(solution)/shard_map/ppermute | solution.py:11
  139.9 9.7 %collective-permute-start.1 = (bf16[128,1152]{1,0:T(8,128)(2,1)}, bf16[128,1152]{1,0:T(8,128)(2,1)S(1)}, u32[]{:S(2)}, u32[]{:S(2)}) collective-permute-start(bf16[128,1152]{1,0:T(8,128)(2,1)} %get-tuple-element.481), channel_id=1, source_target_pairs={{0,31},{1,0},{2,1},{3,2},{4,3},{5,4},{6,5},{7,6},{8,7},{9,8},{10,9... | collective-permute-start | bytes 884744 | tf_op jit(solution)/shard_map/while/body/eval_jaxpr/ppermute | solution.py:11
  142.9 13.2 %collective-permute-start = (bf16[128,1152]{1,0:T(8,128)(2,1)}, bf16[128,1152]{1,0:T(8,128)(2,1)S(1)}, u32[]{:S(2)}, u32[]{:S(2)}) collective-permute-start(bf16[128,1152]{1,0:T(8,128)(2,1)} %get-tuple-element.480), channel_id=1, source_target_pairs={{0,1},{1,2},{2,3},{3,4},{4,5},{5,6},{6,7},{7,8},{8,9},{9,10},{10,1... | collective-permute-start | bytes 884744 | tf_op jit(solution)/shard_map/while/body/eval_jaxpr/ppermute | solution.py:11
  142.9 26.0 %collective-permute-start.2 = (f32[128,1152]{1,0:T(8,128)}, f32[128,1152]{1,0:T(8,128)}, u32[]{:S(2)}, u32[]{:S(2)}) collective-permute-start(f32[128,1152]{1,0:T(8,128)} %get-tuple-element.482), channel_id=1, source_target_pairs={{0,1},{1,2},{2,3},{3,4},{4,5},{5,6},{6,7},{7,8},{8,9},{9,10},{10,1... | collective-permute-start | bytes 1769480 | tf_op jit(solution)/shard_map/while/body/eval_jaxpr/ppermute | solution.py:11
  142.9 38.4 %collective-permute-start.3 = (f32[128,1152]{1,0:T(8,128)}, f32[128,1152]{1,0:T(8,128)}, u32[]{:S(2)}, u32[]{:S(2)}) collective-permute-start(f32[128,1152]{1,0:T(8,128)} %get-tuple-element.483), channel_id=1, source_target_pairs={{0,31},{1,0},{2,1},{3,2},{4,3},{5,4},{6,5},{7,6},{8,7},{9,8},{10,9... | collective-permute-start | bytes 1769480 | tf_op jit(solution)/shard_map/while/body/eval_jaxpr/ppermute | solution.py:11
  148.2 10.3 %copy-start.1 = (f32[128,1152]{1,0:T(8,128)S(1)}, f32[128,1152]{1,0:T(8,128)}, u32[]{:S(2)}) copy-start(f32[128,1152]{1,0:T(8,128)} %get-tuple-element.484) | copy-start | bytes 1769476 | tf_op jit(solution)/shard_map/while
  158.9 24.6 %copy-start.2 = (f32[128,1152]{1,0:T(8,128)}, f32[128,1152]{1,0:T(8,128)S(1)}, u32[]{:S(2)}) copy-start(f32[128,1152]{1,0:T(8,128)S(1)} %fusion.93) | copy-start | bytes 1769476 | tf_op jit(solution)/shard_map/while
  183.4 13.3 %collective-permute-start.1 = (bf16[128,1152]{1,0:T(8,128)(2,1)}, bf16[128,1152]{1,0:T(8,128)(2,1)S(1)}, u32[]{:S(2)}, u32[]{:S(2)}) collective-permute-start(bf16[128,1152]{1,0:T(8,128)(2,1)} %get-tuple-element.481), channel_id=1, source_target_pairs={{0,31},{1,0},{2,1},{3,2},{4,3},{5,4},{6,5},{7,6},{8,7},{9,8},{10,9... | collective-permute-start | bytes 884744 | tf_op jit(solution)/shard_map/while/body/eval_jaxpr/ppermute | solution.py:11
  188.9 14.1 %collective-permute-start = (bf16[128,1152]{1,0:T(8,128)(2,1)}, bf16[128,1152]{1,0:T(8,128)(2,1)S(1)}, u32[]{:S(2)}, u32[]{:S(2)}) collective-permute-start(bf16[128,1152]{1,0:T(8,128)(2,1)} %get-tuple-element.480), channel_id=1, source_target_pairs={{0,1},{1,2},{2,3},{3,4},{4,5},{5,6},{6,7},{7,8},{8,9},{9,10},{10,1... | collective-permute-start | bytes 884744 | tf_op jit(solution)/shard_map/while/body/eval_jaxpr/ppermute | solution.py:11
  188.9 26.9 %collective-permute-start.2 = (f32[128,1152]{1,0:T(8,128)}, f32[128,1152]{1,0:T(8,128)}, u32[]{:S(2)}, u32[]{:S(2)}) collective-permute-start(f32[128,1152]{1,0:T(8,128)} %get-tuple-element.482), channel_id=1, source_target_pairs={{0,1},{1,2},{2,3},{3,4},{4,5},{5,6},{6,7},{7,8},{8,9},{9,10},{10,1... | collective-permute-start | bytes 1769480 | tf_op jit(solution)/shard_map/while/body/eval_jaxpr/ppermute | solution.py:11
  188.9 38.5 %collective-permute-start.3 = (f32[128,1152]{1,0:T(8,128)}, f32[128,1152]{1,0:T(8,128)}, u32[]{:S(2)}, u32[]{:S(2)}) collective-permute-start(f32[128,1152]{1,0:T(8,128)} %get-tuple-element.483), channel_id=1, source_target_pairs={{0,31},{1,0},{2,1},{3,2},{4,3},{5,4},{6,5},{7,6},{8,7},{9,8},{10,9... | collective-permute-start | bytes 1769480 | tf_op jit(solution)/shard_map/while/body/eval_jaxpr/ppermute | solution.py:11
  194.3 11.2 %copy-start.1 = (f32[128,1152]{1,0:T(8,128)S(1)}, f32[128,1152]{1,0:T(8,128)}, u32[]{:S(2)}) copy-start(f32[128,1152]{1,0:T(8,128)} %get-tuple-element.484) | copy-start | bytes 1769476 | tf_op jit(solution)/shard_map/while
  205.9 23.7 %copy-start.2 = (f32[128,1152]{1,0:T(8,128)}, f32[128,1152]{1,0:T(8,128)S(1)}, u32[]{:S(2)}) copy-start(f32[128,1152]{1,0:T(8,128)S(1)} %fusion.93) | copy-start | bytes 1769476 | tf_op jit(solution)/shard_map/while
  229.6 13.2 %collective-permute-start.1 = (bf16[128,1152]{1,0:T(8,128)(2,1)}, bf16[128,1152]{1,0:T(8,128)(2,1)S(1)}, u32[]{:S(2)}, u32[]{:S(2)}) collective-permute-start(bf16[128,1152]{1,0:T(8,128)(2,1)} %get-tuple-element.481), channel_id=1, source_target_pairs={{0,31},{1,0},{2,1},{3,2},{4,3},{5,4},{6,5},{7,6},{8,7},{9,8},{10,9... | collective-permute-start | bytes 884744 | tf_op jit(solution)/shard_map/while/body/eval_jaxpr/ppermute | solution.py:11
  235.1 14.2 %collective-permute-start = (bf16[128,1152]{1,0:T(8,128)(2,1)}, bf16[128,1152]{1,0:T(8,128)(2,1)S(1)}, u32[]{:S(2)}, u32[]{:S(2)}) collective-permute-start(bf16[128,1152]{1,0:T(8,128)(2,1)} %get-tuple-element.480), channel_id=1, source_target_pairs={{0,1},{1,2},{2,3},{3,4},{4,5},{5,6},{6,7},{7,8},{8,9},{9,10},{10,1... | collective-permute-start | bytes 884744 | tf_op jit(solution)/shard_map/while/body/eval_jaxpr/ppermute | solution.py:11
  235.1 26.9 %collective-permute-start.2 = (f32[128,1152]{1,0:T(8,128)}, f32[128,1152]{1,0:T(8,128)}, u32[]{:S(2)}, u32[]{:S(2)}) collective-permute-start(f32[128,1152]{1,0:T(8,128)} %get-tuple-element.482), channel_id=1, source_target_pairs={{0,1},{1,2},{2,3},{3,4},{4,5},{5,6},{6,7},{7,8},{8,9},{9,10},{10,1... | collective-permute-start | bytes 1769480 | tf_op jit(solution)/shard_map/while/body/eval_jaxpr/ppermute | solution.py:11
  235.1 36.7 %collective-permute-start.3 = (f32[128,1152]{1,0:T(8,128)}, f32[128,1152]{1,0:T(8,128)}, u32[]{:S(2)}, u32[]{:S(2)}) collective-permute-start(f32[128,1152]{1,0:T(8,128)} %get-tuple-element.483), channel_id=1, source_target_pairs={{0,31},{1,0},{2,1},{3,2},{4,3},{5,4},{6,5},{7,6},{8,7},{9,8},{10,9... | collective-permute-start | bytes 1769480 | tf_op jit(solution)/shard_map/while/body/eval_jaxpr/ppermute | solution.py:11
  240.5 11.3 %copy-start.1 = (f32[128,1152]{1,0:T(8,128)S(1)}, f32[128,1152]{1,0:T(8,128)}, u32[]{:S(2)}) copy-start(f32[128,1152]{1,0:T(8,128)} %get-tuple-element.484) | copy-start | bytes 1769476 | tf_op jit(solution)/shard_map/while
  252.1 21.9 %copy-start.2 = (f32[128,1152]{1,0:T(8,128)}, f32[128,1152]{1,0:T(8,128)S(1)}, u32[]{:S(2)}) copy-start(f32[128,1152]{1,0:T(8,128)S(1)} %fusion.93) | copy-start | bytes 1769476 | tf_op jit(solution)/shard_map/while
  274.0 13.2 %collective-permute-start.1 = (bf16[128,1152]{1,0:T(8,128)(2,1)}, bf16[128,1152]{1,0:T(8,128)(2,1)S(1)}, u32[]{:S(2)}, u32[]{:S(2)}) collective-permute-start(bf16[128,1152]{1,0:T(8,128)(2,1)} %get-tuple-element.481), channel_id=1, source_target_pairs={{0,31},{1,0},{2,1},{3,2},{4,3},{5,4},{6,5},{7,6},{8,7},{9,8},{10,9... | collective-permute-start | bytes 884744 | tf_op jit(solution)/shard_map/while/body/eval_jaxpr/ppermute | solution.py:11
  279.5 14.1 %collective-permute-start = (bf16[128,1152]{1,0:T(8,128)(2,1)}, bf16[128,1152]{1,0:T(8,128)(2,1)S(1)}, u32[]{:S(2)}, u32[]{:S(2)}) collective-permute-start(bf16[128,1152]{1,0:T(8,128)(2,1)} %get-tuple-element.480), channel_id=1, source_target_pairs={{0,1},{1,2},{2,3},{3,4},{4,5},{5,6},{6,7},{7,8},{8,9},{9,10},{10,1... | collective-permute-start | bytes 884744 | tf_op jit(solution)/shard_map/while/body/eval_jaxpr/ppermute | solution.py:11
  279.5 26.8 %collective-permute-start.2 = (f32[128,1152]{1,0:T(8,128)}, f32[128,1152]{1,0:T(8,128)}, u32[]{:S(2)}, u32[]{:S(2)}) collective-permute-start(f32[128,1152]{1,0:T(8,128)} %get-tuple-element.482), channel_id=1, source_target_pairs={{0,1},{1,2},{2,3},{3,4},{4,5},{5,6},{6,7},{7,8},{8,9},{9,10},{10,1... | collective-permute-start | bytes 1769480 | tf_op jit(solution)/shard_map/while/body/eval_jaxpr/ppermute | solution.py:11
  279.5 35.0 %collective-permute-start.3 = (f32[128,1152]{1,0:T(8,128)}, f32[128,1152]{1,0:T(8,128)}, u32[]{:S(2)}, u32[]{:S(2)}) collective-permute-start(f32[128,1152]{1,0:T(8,128)} %get-tuple-element.483), channel_id=1, source_target_pairs={{0,31},{1,0},{2,1},{3,2},{4,3},{5,4},{6,5},{7,6},{8,7},{9,8},{10,9... | collective-permute-start | bytes 1769480 | tf_op jit(solution)/shard_map/while/body/eval_jaxpr/ppermute | solution.py:11
  284.9 11.2 %copy-start.1 = (f32[128,1152]{1,0:T(8,128)S(1)}, f32[128,1152]{1,0:T(8,128)}, u32[]{:S(2)}) copy-start(f32[128,1152]{1,0:T(8,128)} %get-tuple-element.484) | copy-start | bytes 1769476 | tf_op jit(solution)/shard_map/while
  296.4 20.2 %copy-start.2 = (f32[128,1152]{1,0:T(8,128)}, f32[128,1152]{1,0:T(8,128)S(1)}, u32[]{:S(2)}) copy-start(f32[128,1152]{1,0:T(8,128)S(1)} %fusion.93) | copy-start | bytes 1769476 | tf_op jit(solution)/shard_map/while
  316.6 13.2 %collective-permute-start.1 = (bf16[128,1152]{1,0:T(8,128)(2,1)}, bf16[128,1152]{1,0:T(8,128)(2,1)S(1)}, u32[]{:S(2)}, u32[]{:S(2)}) collective-permute-start(bf16[128,1152]{1,0:T(8,128)(2,1)} %get-tuple-element.481), channel_id=1, source_target_pairs={{0,31},{1,0},{2,1},{3,2},{4,3},{5,4},{6,5},{7,6},{8,7},{9,8},{10,9... | collective-permute-start | bytes 884744 | tf_op jit(solution)/shard_map/while/body/eval_jaxpr/ppermute | solution.py:11
  322.1 14.1 %collective-permute-start = (bf16[128,1152]{1,0:T(8,128)(2,1)}, bf16[128,1152]{1,0:T(8,128)(2,1)S(1)}, u32[]{:S(2)}, u32[]{:S(2)}) collective-permute-start(bf16[128,1152]{1,0:T(8,128)(2,1)} %get-tuple-element.480), channel_id=1, source_target_pairs={{0,1},{1,2},{2,3},{3,4},{4,5},{5,6},{6,7},{7,8},{8,9},{9,10},{10,1... | collective-permute-start | bytes 884744 | tf_op jit(solution)/shard_map/while/body/eval_jaxpr/ppermute | solution.py:11
  322.1 26.7 %collective-permute-start.2 = (f32[128,1152]{1,0:T(8,128)}, f32[128,1152]{1,0:T(8,128)}, u32[]{:S(2)}, u32[]{:S(2)}) collective-permute-start(f32[128,1152]{1,0:T(8,128)} %get-tuple-element.482), channel_id=1, source_target_pairs={{0,1},{1,2},{2,3},{3,4},{4,5},{5,6},{6,7},{7,8},{8,9},{9,10},{10,1... | collective-permute-start | bytes 1769480 | tf_op jit(solution)/shard_map/while/body/eval_jaxpr/ppermute | solution.py:11
  322.1 33.8 %collective-permute-start.3 = (f32[128,1152]{1,0:T(8,128)}, f32[128,1152]{1,0:T(8,128)}, u32[]{:S(2)}, u32[]{:S(2)}) collective-permute-start(f32[128,1152]{1,0:T(8,128)} %get-tuple-element.483), channel_id=1, source_target_pairs={{0,31},{1,0},{2,1},{3,2},{4,3},{5,4},{6,5},{7,6},{8,7},{9,8},{10,9... | collective-permute-start | bytes 1769480 | tf_op jit(solution)/shard_map/while/body/eval_jaxpr/ppermute | solution.py:11
  327.5 11.2 %copy-start.1 = (f32[128,1152]{1,0:T(8,128)S(1)}, f32[128,1152]{1,0:T(8,128)}, u32[]{:S(2)}) copy-start(f32[128,1152]{1,0:T(8,128)} %get-tuple-element.484) | copy-start | bytes 1769476 | tf_op jit(solution)/shard_map/while
  339.0 19.1 %copy-start.2 = (f32[128,1152]{1,0:T(8,128)}, f32[128,1152]{1,0:T(8,128)S(1)}, u32[]{:S(2)}) copy-start(f32[128,1152]{1,0:T(8,128)S(1)} %fusion.93) | copy-start | bytes 1769476 | tf_op jit(solution)/shard_map/while
  358.1 12.6 %collective-permute-start.1 = (bf16[128,1152]{1,0:T(8,128)(2,1)}, bf16[128,1152]{1,0:T(8,128)(2,1)S(1)}, u32[]{:S(2)}, u32[]{:S(2)}) collective-permute-start(bf16[128,1152]{1,0:T(8,128)(2,1)} %get-tuple-element.481), channel_id=1, source_target_pairs={{0,31},{1,0},{2,1},{3,2},{4,3},{5,4},{6,5},{7,6},{8,7},{9,8},{10,9... | collective-permute-start | bytes 884744 | tf_op jit(solution)/shard_map/while/body/eval_jaxpr/ppermute | solution.py:11
  363.0 14.1 %collective-permute-start = (bf16[128,1152]{1,0:T(8,128)(2,1)}, bf16[128,1152]{1,0:T(8,128)(2,1)S(1)}, u32[]{:S(2)}, u32[]{:S(2)}) collective-permute-start(bf16[128,1152]{1,0:T(8,128)(2,1)} %get-tuple-element.480), channel_id=1, source_target_pairs={{0,1},{1,2},{2,3},{3,4},{4,5},{5,6},{6,7},{7,8},{8,9},{9,10},{10,1... | collective-permute-start | bytes 884744 | tf_op jit(solution)/shard_map/while/body/eval_jaxpr/ppermute | solution.py:11
  363.0 26.8 %collective-permute-start.2 = (f32[128,1152]{1,0:T(8,128)}, f32[128,1152]{1,0:T(8,128)}, u32[]{:S(2)}, u32[]{:S(2)}) collective-permute-start(f32[128,1152]{1,0:T(8,128)} %get-tuple-element.482), channel_id=1, source_target_pairs={{0,1},{1,2},{2,3},{3,4},{4,5},{5,6},{6,7},{7,8},{8,9},{9,10},{10,1... | collective-permute-start | bytes 1769480 | tf_op jit(solution)/shard_map/while/body/eval_jaxpr/ppermute | solution.py:11
  363.0 36.2 %collective-permute-start.3 = (f32[128,1152]{1,0:T(8,128)}, f32[128,1152]{1,0:T(8,128)}, u32[]{:S(2)}, u32[]{:S(2)}) collective-permute-start(f32[128,1152]{1,0:T(8,128)} %get-tuple-element.483), channel_id=1, source_target_pairs={{0,31},{1,0},{2,1},{3,2},{4,3},{5,4},{6,5},{7,6},{8,7},{9,8},{10,9... | collective-permute-start | bytes 1769480 | tf_op jit(solution)/shard_map/while/body/eval_jaxpr/ppermute | solution.py:11
  368.4 11.2 %copy-start.1 = (f32[128,1152]{1,0:T(8,128)S(1)}, f32[128,1152]{1,0:T(8,128)}, u32[]{:S(2)}) copy-start(f32[128,1152]{1,0:T(8,128)} %get-tuple-element.484) | copy-start | bytes 1769476 | tf_op jit(solution)/shard_map/while
  379.9 21.5 %copy-start.2 = (f32[128,1152]{1,0:T(8,128)}, f32[128,1152]{1,0:T(8,128)S(1)}, u32[]{:S(2)}) copy-start(f32[128,1152]{1,0:T(8,128)S(1)} %fusion.93) | copy-start | bytes 1769476 | tf_op jit(solution)/shard_map/while
  401.4 10.6 %collective-permute-start.1 = (bf16[128,1152]{1,0:T(8,128)(2,1)}, bf16[128,1152]{1,0:T(8,128)(2,1)S(1)}, u32[]{:S(2)}, u32[]{:S(2)}) collective-permute-start(bf16[128,1152]{1,0:T(8,128)(2,1)} %get-tuple-element.481), channel_id=1, source_target_pairs={{0,31},{1,0},{2,1},{3,2},{4,3},{5,4},{6,5},{7,6},{8,7},{9,8},{10,9... | collective-permute-start | bytes 884744 | tf_op jit(solution)/shard_map/while/body/eval_jaxpr/ppermute | solution.py:11
  403.5 14.2 %collective-permute-start = (bf16[128,1152]{1,0:T(8,128)(2,1)}, bf16[128,1152]{1,0:T(8,128)(2,1)S(1)}, u32[]{:S(2)}, u32[]{:S(2)}) collective-permute-start(bf16[128,1152]{1,0:T(8,128)(2,1)} %get-tuple-element.480), channel_id=1, source_target_pairs={{0,1},{1,2},{2,3},{3,4},{4,5},{5,6},{6,7},{7,8},{8,9},{9,10},{10,1... | collective-permute-start | bytes 884744 | tf_op jit(solution)/shard_map/while/body/eval_jaxpr/ppermute | solution.py:11
  403.5 26.9 %collective-permute-start.2 = (f32[128,1152]{1,0:T(8,128)}, f32[128,1152]{1,0:T(8,128)}, u32[]{:S(2)}, u32[]{:S(2)}) collective-permute-start(f32[128,1152]{1,0:T(8,128)} %get-tuple-element.482), channel_id=1, source_target_pairs={{0,1},{1,2},{2,3},{3,4},{4,5},{5,6},{6,7},{7,8},{8,9},{9,10},{10,1... | collective-permute-start | bytes 1769480 | tf_op jit(solution)/shard_map/while/body/eval_jaxpr/ppermute | solution.py:11
  405.2 36.4 %collective-permute-start.3 = (f32[128,1152]{1,0:T(8,128)}, f32[128,1152]{1,0:T(8,128)}, u32[]{:S(2)}, u32[]{:S(2)}) collective-permute-start(f32[128,1152]{1,0:T(8,128)} %get-tuple-element.483), channel_id=1, source_target_pairs={{0,31},{1,0},{2,1},{3,2},{4,3},{5,4},{6,5},{7,6},{8,7},{9,8},{10,9... | collective-permute-start | bytes 1769480 | tf_op jit(solution)/shard_map/while/body/eval_jaxpr/ppermute | solution.py:11
  408.9 11.3 %copy-start.1 = (f32[128,1152]{1,0:T(8,128)S(1)}, f32[128,1152]{1,0:T(8,128)}, u32[]{:S(2)}) copy-start(f32[128,1152]{1,0:T(8,128)} %get-tuple-element.484) | copy-start | bytes 1769476 | tf_op jit(solution)/shard_map/while
  420.5 23.2 %copy-start.2 = (f32[128,1152]{1,0:T(8,128)}, f32[128,1152]{1,0:T(8,128)S(1)}, u32[]{:S(2)}) copy-start(f32[128,1152]{1,0:T(8,128)S(1)} %fusion.93) | copy-start | bytes 1769476 | tf_op jit(solution)/shard_map/while
  443.8 49.8 %copy-start.10 = (f32[128]{0:T(128)}, f32[128]{0:T(128)S(1)}, u32[]{:S(2)}) copy-start(f32[128]{0:T(128)S(1)} %get-tuple-element.319) | copy-start | bytes 1540
  443.8 48.3 %copy-start.4 = (f32[128,2304]{1,0:T(8,128)S(1)}, f32[128,2304]{1,0:T(8,128)}, u32[]{:S(2)}) copy-start(f32[128,2304]{1,0:T(8,128)} %reduce-scatter.2.cloned.1.call-done) | copy-start | bytes 3538948
  443.8 15.2 %collective-permute-start.6 = (f32[128,1152]{1,0:T(8,128)}, f32[128,1152]{1,0:T(8,128)S(1)}, u32[]{:S(2)}, u32[]{:S(2)}) collective-permute-start(f32[128,1152]{1,0:T(8,128)} %get-tuple-element.322), channel_id=1, source_target_pairs={{0,31},{1,0},{2,1},{3,2},{4,3},{5,4},{6,5},{7,6},{8,7},{9,8},{10,9... | collective-permute-start | bytes 1769480 | tf_op jit(solution)/shard_map/ppermute | solution.py:11
  459.0 34.6 %copy-start.3 = (f32[128,1152]{1,0:T(8,128)S(1)}, f32[128,1152]{1,0:T(8,128)}, u32[]{:S(2)}) copy-start(f32[128,1152]{1,0:T(8,128)} %get-tuple-element.320) | copy-start | bytes 1769476
  459.0 34.6 %copy-start.6 = (bf16[128,1152]{1,0:T(8,128)(2,1)S(1)}, bf16[128,1152]{1,0:T(8,128)(2,1)}, u32[]{:S(2)}) copy-start(bf16[128,1152]{1,0:T(8,128)(2,1)} %param.13) | copy-start | bytes 884740
  460.2 15.8 %collective-permute-start.7 = (f32[128,1152]{1,0:T(8,128)S(1)}, f32[128,1152]{1,0:T(8,128)S(1)}, u32[]{:S(2)}, u32[]{:S(2)}) collective-permute-start(f32[128,1152]{1,0:T(8,128)S(1)} %add.355), channel_id=1, source_target_pairs={{0,25},{1,26},{2,27},{3,28},{4,29},{5,30},{6,31},{7,0},{8,1},{9,2}... | collective-permute-start | bytes 1769480 | tf_op jit(solution)/shard_map/ppermute | solution.py:11
  476.0 16.1 %collective-permute-start.8 = (f32[128,1152]{1,0:T(8,128)S(1)}, f32[128,1152]{1,0:T(8,128)S(1)}, u32[]{:S(2)}, u32[]{:S(2)}) collective-permute-start(f32[128,1152]{1,0:T(8,128)S(1)} %collective-permute-done.7), channel_id=1, source_target_pairs={{0,16},{1,17},{2,18},{3,19},{4,20},{5,21},{6,22},{7,23},{8,24},{9,... | collective-permute-start | bytes 1769480 | tf_op jit(solution)/shard_map/ppermute | solution.py:11
Sparse Core Ops, SparseCore 0:
  15.5 88.0 reduce-scatter.1
where the time goes:
time: 503 us; the launch traced here: 502 us
  waiting for transfers between devices  328 us (65%)
  starting transfers between devices  76.7 us (15%)
  matrix products  56.6 us (11%)
  between operations  16.2 us (3%)
  local copies, waits for them, and re-layouts  12.5 us (2%)
  other arithmetic  11.5 us (2%)
    ppermute x33, waiting for transfers between devices, shifted(): lax.ppermute(shard, axis, [(i, (i + by) % devices) for i in range(devices)])  240 us
    reduce_scatter x1, waiting for transfers between devices, body(): lax.psum_scatter(jnp.concatenate([jnp.dot(img_hidden, img_down, preferred...  88.2 us
    ppermute x33, starting transfers between devices, shifted(): lax.ppermute(shard, axis, [(i, (i + by) % devices) for i in range(devices)])  76.7 us
    dot_general x16, matrix products, pair_tile(): lax.dot_general(coef, image_low, (((0,), (0,)), ((), ())), preferred_elem...  32.5 us
    dot_general x16, matrix products, pair_tile(): lax.dot_general(image_low, text_block, (((1,), (1,)), ((), ())), preferre...  13.7 us
  transfers between devices with their start and end apart: 34, of which 34 were waited for; matrix products, arithmetic and copies ran while one was open for 9% of the time, Pallas kernels for 0%

commit v1 on v0

--- a/solution.py
+++ b/solution.py
@@ -51,7 +51,7 @@
     return text_sum
 
 
-def body(
+def ring_body(
     img_hidden, img_down, img_pooled, txt_hidden, txt_proj, log_temp, bias, match, window_index
 ):
     width = img_pooled.shape[1]
@@ -144,6 +144,73 @@
     return (img_grad, txt_grad, row_loss)
 
 
+def scatter_sum(partial, axis):
+    parts = lax.axis_size(axis)
+    rows = partial.shape[0] // parts
+    pieces = partial.astype(jnp.bfloat16).reshape(parts, rows, partial.shape[1])
+    got = lax.all_to_all(pieces, axis, 0, 0).astype(jnp.float32)
+    return jnp.sum(got, axis=0)
+
+
+def stable_terms(logit, positive):
+    signed = jnp.where(positive, -logit, logit)
+    small = jnp.exp(-jnp.abs(signed))
+    loss = jnp.maximum(signed, 0.0) + jnp.log1p(small)
+    chance = jnp.where(signed >= 0.0, 1.0, small) / (1.0 + small)
+    return loss, jnp.where(positive, -chance, chance)
+
+
+def tangent(dunit, unit, length):
+    return (dunit - unit * jnp.sum(unit * dunit, axis=1, keepdims=True)) / length
+
+
+def gather_body(
+    img_hidden, img_down, img_pooled, txt_hidden, txt_proj, log_temp, bias, match, window_index
+):
+    both = ("dp", "tensor")
+    width = img_pooled.shape[1]
+    rows = img_pooled.shape[0]
+    devices = lax.axis_size(both)
+    position = lax.axis_index(both)
+    txt_emb = scatter_sum(jnp.dot(txt_hidden, txt_proj, preferred_element_type=jnp.float32), "tensor")
+    img_emb = scatter_sum(
+        jnp.dot(img_hidden, img_down, preferred_element_type=jnp.float32), "tensor"
+    ) + img_pooled.astype(jnp.float32)
+    img_unit, img_len = unit_rows(img_emb)
+    txt_unit, txt_len = unit_rows(txt_emb)
+    image_low = img_unit.astype(jnp.bfloat16)
+    text_low = txt_unit.astype(jnp.bfloat16)
+    texts = lax.all_gather(text_low, both, axis=0, tiled=True)
+    images = lax.all_gather(image_low, both, axis=0, tiled=True)
+    matches = lax.all_gather(match, both, axis=0, tiled=True)
+    scale = jnp.exp(log_temp[0])
+    shift_value = bias[0]
+    window = window_index[0]
+    every = lax.iota(jnp.int32, devices * rows)
+    own = position * rows + lax.iota(jnp.int32, rows)
+    nt = (((1,), (1,)), ((), ()))
+
+    logit = scale * lax.dot_general(image_low, texts, nt, preferred_element_type=jnp.float32) + shift_value
+    offset = (position - every // rows) % devices
+    inside = (offset // STEPS == window)[None, :]
+    loss, slope = stable_terms(logit, match[:, None] == every[None, :])
+    row_loss = jnp.sum(jnp.where(inside, loss, 0.0), axis=1)
+    coef = jnp.where(inside, slope * scale, 0.0).astype(jnp.bfloat16)
+    image_dunit = jnp.dot(coef, texts, preferred_element_type=jnp.float32)
+
+    logit = scale * lax.dot_general(text_low, images, nt, preferred_element_type=jnp.float32) + shift_value
+    offset = (every // rows - position) % devices
+    inside = (offset // STEPS == window)[None, :]
+    _, slope = stable_terms(logit, matches[None, :] == own[:, None])
+    coef = jnp.where(inside, slope * scale, 0.0).astype(jnp.bfloat16)
+    text_dunit = jnp.dot(coef, images, preferred_element_type=jnp.float32)
+    return (
+        tangent(image_dunit, img_unit, img_len),
+        tangent(text_dunit, txt_unit, txt_len),
+        row_loss,
+    )
+
+
 def solution(mesh):
     in_specs = (
         P("dp", "tensor"),
@@ -157,4 +224,6 @@
         P(),
     )
     out_specs = (P(("dp", "tensor"), None), P(("dp", "tensor"), None), P(("dp", "tensor")))
+    whole = mesh.shape["dp"] * mesh.shape["tensor"]
+    body = gather_body if whole <= 2 * STEPS else ring_body
     return jax.shard_map(body, mesh=mesh, in_specs=in_specs, out_specs=out_specs, check_vma=False)

time: 503 us -> 239 us (0.48)
  waiting for transfers between devices: 328 us -> 39.4 us
  blocking collectives: 0 us -> 147 us
  starting transfers between devices: 76.7 us -> 0.08 us
  matrix products: 56.6 us -> 27.9 us
  local copies, waits for them, and re-layouts: 12.5 us -> 2.35 us
  other arithmetic: 11.5 us -> 5.55 us
    ppermute x33 -> x0, waiting for transfers between devices: 240 us -> none  [shifted(): lax.ppermute(shard, axis, [(i, (i + by) % devices) for i in range(devices)])]
    reduce_scatter x1 -> x0, waiting for transfers between devices: 88.2 us -> none  [body(): lax.psum_scatter(jnp.concatenate([jnp.dot(img_hidden, img_down, preferred...]
    all_to_all x0 -> x2, blocking collectives: none -> 82.2 us  [scatter_sum(): got = lax.all_to_all(pieces, axis, 0, 0).astype(jnp.float32)]
    ppermute x33 -> x0, starting transfers between devices: 76.7 us -> none  [shifted(): lax.ppermute(shard, axis, [(i, (i + by) % devices) for i in range(devices)])]
    all_gather x0 -> x1, blocking collectives: none -> 64.8 us  [gather_body(): matches = lax.all_gather(match, both, axis=0, tiled=True)]
    all_gather x0 -> x2, waiting for transfers between devices: none -> 39.4 us  [the longest x1 39.3 us: gather_body(): texts = lax.all_gather(text_low, both, axis=0, tiled=True)]
    dot_general x50 -> x5, matrix products: 56.6 us -> 27.9 us  [the longest x1 12.4 us: gather_body(): text_dunit = jnp.dot(coef, images, preferred_element_type=jnp.float32)]
    while x42 -> x0, local copies, waits for them, and re-layouts: 9.97 us -> none
  transfers between devices with their start and end apart: 34 -> 2, of which waited for: 34 -> 1; matrix products, arithmetic and copies ran while one was open for 9% -> 7% of each run, Pallas kernels for 0% -> 0%
where the time goes in v1:
time: 239 us; the launch traced here: 238 us
  blocking collectives  147 us (62%)
  waiting for transfers between devices  39.4 us (16%)
  matrix products  27.9 us (12%)
  between operations  16.1 us (7%)
  other arithmetic  5.55 us (2%)
    all_to_all x2, blocking collectives, scatter_sum(): got = lax.all_to_all(pieces, axis, 0, 0).astype(jnp.float32)  82.2 us
    all_gather x1, blocking collectives, gather_body(): matches = lax.all_gather(match, both, axis=0, tiled=True)  64.8 us
    all_gather x1, waiting for transfers between devices, gather_body(): texts = lax.all_gather(text_low, both, axis=0, tiled=True)  39.3 us
    dot_general x1, matrix products, gather_body(): text_dunit = jnp.dot(coef, images, preferred_element_type=jnp.float32)  12.4 us
    dot_general x1, matrix products, gather_body(): lax.dot_general(image_low, texts, nt, preferred_element_type=jnp.float32)  8.27 us
  transfers between devices with their start and end apart: 2, of which 1 were waited for; matrix products, arithmetic and copies ran while one was open for 7% of the time, Pallas kernels for 0%

profile of v1, /device:TPU:0, one launch (start us, length us, event | category | flops | bytes accessed | tf_op | source)
XLA Modules:
  0.0 238.4 jit_solution(3820518135389666020)
XLA Ops:
  7.2 0.0 copy-start
  7.2 0.0 all-gather.6.cloned.1.call-start
  7.2 1.6 copy-done
  8.9 3.1 %convolution_convert_fusion.1 = bf16[512,1152]{1,0:T(8,128)(2,1)S(1)} fusion(bf16[512,1076]{0,1:T(8,128)(2,1)} %param.9, bf16[1076,1152]{1,0:T(8,128)(2,1)S(1)} %copy-done), kind=kOutput, calls=%fused_computation.9 | convolution fusion | flops 1269891072 | bytes 4760576 | tf_op jit(solution)/shard_map/dot_general | solution.py:177
  12.0 0.0 copy-start.2
  12.0 34.8 %all_to_all.10 = bf16[4,128,1152]{2,1,0:T(8,128)(2,1)S(1)} all-to-all(bf16[4,128,1152]{2,1,0:T(8,128)(2,1)S(1)} %bitcast.21), channel_id=1, replica_groups=mesh['dp'=8,'tensor'=4] {'tensor'}, dimensions={0} | all-to-all | bytes 2359296 | tf_op jit(solution)/shard_map/all_to_all | solution.py:151
  46.8 0.2 convert_reduce_fusion.1
  47.0 0.0 copy-done.2
  47.0 0.2 multiply_reduce_fusion.3
  47.2 0.9 fusion.42
  48.0 0.0 all-gather.6.cloned.1.call-update
  48.0 0.0 all-gather.4.cloned.1.call-start
  48.1 2.0 convolution_convert_fusion
  50.1 47.4 %all_to_all.11 = bf16[4,128,1152]{2,1,0:T(8,128)(2,1)S(1)} all-to-all(bf16[4,128,1152]{2,1,0:T(8,128)(2,1)S(1)} %bitcast.22), channel_id=1, replica_groups=mesh['dp'=8,'tensor'=4] {'tensor'}, dimensions={0} | all-to-all | bytes 2359296 | tf_op jit(solution)/shard_map/all_to_all | solution.py:151
  97.6 0.0 copy-start.3
  97.6 0.2 convert_reduce_fusion
  97.7 0.0 copy-start.1
  97.7 0.1 multiply_reduce_fusion.2
  97.9 0.7 copy-done.1
  98.5 0.8 fusion.41
  99.4 0.0 all-gather.4.cloned.1.call-update
  101.4 0.0 copy-done.3
  101.4 64.8 %all-gather = s32[32,1,128]{2,1,0:T(1,128)S(1)} all-gather(s32[1,1,128]{2,1,0:T(1,128)S(1)} %bitcast.24), channel_id=1, replica_groups=mesh['dp'=8,'tensor'=4] {'dp','tensor'}, dimensions={0}, use_global_device_ids=true | all-gather | bytes 16896 | tf_op jit(solution)/shard_map/all_gather | solution.py:185
  166.3 0.0 all-gather.6.cloned.1.call-done
  166.3 12.4 %multiply_reduce_fusion = (f32[128]{0:T(128)S(1)}, f32[128,1152]{1,0:T(8,128)}) fusion(f32[128,1152]{1,0:T(8,128)} %copy-done.1, f32[128]{0:T(128)S(1)} %add_sqrt_fusion, bf16[4096,1152]{1,0:T(8,128)(2,1)} %all-gather.6.cloned.1.call-done, bf16[128,1152]{1,0:T(8,128)(2,1)} %fusion.41, s32[4096]{0:T(1024)S(1)} %bitcast.23, f32[]{:T(128)} %bitcast.18, ...), kind=kOutput, calls=%fused_computation.36 | convolution fusion | flops 2424750080 | bytes 10933768 | tf_op jit(solution)/shard_map/dot_general | solution.py:206
  178.7 2.2 subtract_divide_fusion
  180.9 39.3 %all-gather.4.cloned.1.call-done = bf16[4096,1152]{1,0:T(8,128)(2,1)} async-done(((bf16[128,1152]{1,0:T(8,128)(2,1)}), bf16[4096,1152]{1,0:T(8,128)(2,1)}) %all-gather.4.cloned.1.call-update) | async-done | bytes 9437200 | tf_op jit(solution)/shard_map/all_gather | solution.py:183
  220.2 0.0 copy-start.4
  220.2 8.3 %select_reduce_fusion = (f32[128]{0:T(128)}, f32[128,4096]{1,0:T(8,128)S(1)}) fusion(pred[4096]{0:T(1024)(128)(4,1)S(1)} %fusion.26, f32[]{:T(128)} %bitcast.17, bf16[128,1152]{1,0:T(8,128)(2,1)} %fusion.42, bf16[4096,1152]{1,0:T(8,128)(2,1)} %all-gather.4.cloned.1.call-done, f32[]{:T(128)} %bitcast.1, s32[128]{0:T(128)S(1)} %copy-done.3), kind=kOutput, calls=%fused_computation.18 | convolution fusion | flops 1213726592 | bytes 11834376 | tf_op jit(solution)/shard_map/dot_general | solution.py:193
  228.5 0.0 copy-done.4
  228.5 2.1 multiply_reduce_fusion.1
  230.6 1.0 subtract_divide_fusion.1
  (5 shorter events, 0.1 us)
Async XLA Ops:
  7.2 1.7 copy-start
  7.2 159.1 %all-gather.6.cloned.1.call-start = ((), (), s32[]{:S(2)}) async-start(), calls=%async_computation.3 | async-start | bytes 9732096 | tf_op jit(solution)/shard_map/all_gather | solution.py:184
  12.0 35.0 %copy-start.2 = (bf16[128,1152]{1,0:T(8,128)(2,1)S(1)}, bf16[128,1152]{1,0:T(8,128)(2,1)}, u32[]{:S(2)}) copy-start(bf16[128,1152]{1,0:T(8,128)(2,1)} %param.11) | copy-start | bytes 884740
  48.0 172.2 %all-gather.4.cloned.1.call-start = ((), (), s32[]{:S(2)}) async-start(), calls=%async_computation.2 | async-start | bytes 9732096 | tf_op jit(solution)/shard_map/all_gather | solution.py:183
  97.6 3.8 %copy-start.3 = (s32[128]{0:T(128)S(1)}, s32[128]{0:T(128)}, u32[]{:S(2)}) copy-start(s32[128]{0:T(128)} %param.16) | copy-start | bytes 1540
  97.7 0.8 copy-start.1
  220.2 8.3 %copy-start.4 = (bf16[4096,1152]{1,0:T(8,128)(2,1)S(1)}, bf16[4096,1152]{1,0:T(8,128)(2,1)}, u32[]{:S(2)}) copy-start(bf16[4096,1152]{1,0:T(8,128)(2,1)} %all-gather.4.cloned.1.call-done) | copy-start | bytes 28311556
Sparse Core Ops, SparseCore 0:
  48.2 89.1 all-gather.5
  140.1 80.0 all-gather.3

commit v2 on v1

--- a/solution.py
+++ b/solution.py
@@ -1,6 +1,8 @@
 import jax
 import jax.numpy as jnp
 from jax import lax
+from jax.experimental import pallas as pl
+from jax.experimental.pallas import tpu as pltpu
 from jax.sharding import PartitionSpec as P
 
 STEPS = 16
@@ -164,6 +166,272 @@
     return (dunit - unit * jnp.sum(unit * dunit, axis=1, keepdims=True)) / length
 
 
+def exchange(pay, out, twin, col, z_send, z_recv, p_send, f_send, out_recv, twin_recv, local_sem):
+    dp = lax.axis_index("dp")
+    z = lax.axis_index("tensor")
+    depth = lax.axis_size("tensor")
+    devices = lax.axis_size("dp") * depth
+    half = devices // 2
+    y, x, c = dp // 4, (dp // 2) % 2, dp % 2
+
+    def group(y, x, c):
+        return y * 4 + x * 2 + c
+
+    def slot(kind, source, target):
+        ahead = (1 - 2 * kind) * (target - source)
+        return kind * (half - 1) + lax.rem(ahead + devices, devices) - 1
+
+    peers = [
+        group(y, x, 1 - c),
+        group(y, 1 - x, c),
+        group(1 - y, 1 - x, c),
+        group(1 - y, x, 1 - c),
+        group(1 - y, x, c),
+    ]
+    barrier = pltpu.get_barrier_semaphore()
+    for peer in peers:
+        pl.semaphore_signal(barrier, inc=1, device_id=(peer, z), device_id_type=pl.DeviceIdType.MESH)
+    has_up = z < depth - 1
+    has_down = z > 0
+
+    @pl.when(has_up)
+    def _():
+        pl.semaphore_signal(barrier, inc=1, device_id=(dp, z + 1), device_id_type=pl.DeviceIdType.MESH)
+
+    @pl.when(has_down)
+    def _():
+        pl.semaphore_signal(barrier, inc=1, device_id=(dp, z - 1), device_id_type=pl.DeviceIdType.MESH)
+
+    inner = jnp.logical_and(has_up, has_down)
+
+    @pl.when(inner)
+    def _():
+        pl.semaphore_wait(barrier, len(peers) + 2)
+
+    @pl.when(jnp.logical_not(inner))
+    def _():
+        pl.semaphore_wait(barrier, len(peers) + 1)
+
+    started = []
+
+    def start(condition, make):
+        @pl.when(condition)
+        def _():
+            make().start()
+
+        started.append((condition, make))
+
+    def remote(source, target, send, recv, peer, level):
+        return lambda: pltpu.make_async_remote_copy(
+            src_ref=source(),
+            dst_ref=target(),
+            send_sem=send(),
+            recv_sem=recv(),
+            device_id=(peer, level),
+            device_id_type=pl.DeviceIdType.MESH,
+        )
+
+    def arrived(condition, index):
+        @pl.when(condition)
+        def _():
+            pltpu.make_async_remote_copy(
+                src_ref=out.at[index],
+                dst_ref=out.at[index],
+                send_sem=f_send.at[0, 0],
+                recv_sem=out_recv.at[index],
+                device_id=(peers[0], z),
+                device_id_type=pl.DeviceIdType.MESH,
+            ).wait_recv()
+
+    def along(tag, level, kind, way, condition):
+        held = (lambda: pay.at[kind]) if tag == 0 else (lambda: col.at[level, kind])
+        start(
+            condition,
+            remote(
+                held,
+                lambda: col.at[level, kind],
+                lambda: z_send.at[tag, kind, way],
+                lambda: z_recv.at[level, kind],
+                dp,
+                z + 1 - 2 * way,
+            ),
+        )
+
+    def spread(tag, level, condition):
+        source = dp * depth + level
+
+        def send(job, kind, peer, when):
+            index = slot(kind, source, peer * depth + z)
+            held = (lambda: pay.at[kind]) if tag == 0 else (lambda: col.at[level, kind])
+            start(
+                when,
+                remote(
+                    held,
+                    lambda: out.at[index],
+                    lambda: p_send.at[tag, job],
+                    lambda: out_recv.at[index],
+                    peer,
+                    z,
+                ),
+            )
+
+        send(0, 1 - c, peers[3], condition)
+        send(1, 1 - x, peers[2], condition)
+        send(2, x, peers[1], condition)
+        send(3, c, peers[0], condition)
+        if tag == 0:
+            for kind in (0, 1):
+                start(
+                    condition,
+                    remote(
+                        lambda kind=kind: pay.at[kind],
+                        lambda kind=kind: twin.at[kind],
+                        lambda kind=kind: p_send.at[0, 4 + kind],
+                        lambda kind=kind: twin_recv.at[kind],
+                        peers[4],
+                        z,
+                    ),
+                )
+        else:
+            below = tag % 2
+            send(4, c, peers[4], jnp.logical_and(condition, c == below))
+
+    def keep(tag, level, condition):
+        kind = 1 - tag % 2
+        index = slot(kind, dp * depth + level, dp * depth + z)
+
+        @pl.when(condition)
+        def _():
+            pltpu.make_async_copy(col.at[level, kind], out.at[index], local_sem.at[tag]).start()
+
+    def kept(tag, level, condition):
+        kind = 1 - tag % 2
+        index = slot(kind, dp * depth + level, dp * depth + z)
+
+        @pl.when(condition)
+        def _():
+            pltpu.make_async_copy(col.at[level, kind], out.at[index], local_sem.at[tag]).wait()
+
+    def relay(tag, level, condition):
+        me = dp * depth + z
+        other = peers[0] * depth + z
+
+        def hand(job, kind, origin, when, onward):
+            source = origin * depth + level
+            arrived(when, slot(kind, source, me))
+            if onward is not None:
+                index = slot(kind, source, me)
+                landing = slot(kind, source, other)
+                start(
+                    onward,
+                    remote(
+                        lambda: out.at[index],
+                        lambda: out.at[landing],
+                        lambda: f_send.at[tag, job],
+                        lambda: out_recv.at[landing],
+                        peers[0],
+                        z,
+                    ),
+                )
+
+        hand(0, 1 - x, peers[1], condition, condition)
+        hand(1, x, peers[2], condition, condition)
+        onward = None if tag == 0 else jnp.logical_and(condition, c == tag % 2)
+        hand(2, c, peers[3], condition, onward)
+
+    def finish(tag, level, condition):
+        me = dp * depth + z
+        arrived(condition, slot(1 - c, peers[0] * depth + level, me))
+        arrived(condition, slot(1 - x, group(y, 1 - x, 1 - c) * depth + level, me))
+        arrived(condition, slot(x, group(1 - y, 1 - x, 1 - c) * depth + level, me))
+        if tag:
+            arrived(condition, slot(tag % 2, peers[4] * depth + level, me))
+
+    always = z >= 0
+    for kind in (0, 1):
+        along(0, z, kind, 0, has_up)
+        along(0, z, kind, 1, has_down)
+    spread(0, z, always)
+    turns = [(0, z, always)]
+    for hop in range(1, depth):
+        here = []
+        for way in (0, 1):
+            level = z - hop if way == 0 else z + hop
+            condition = level >= 0 if way == 0 else level < depth
+            tag = 2 * hop - 1 if way == 0 else 2 * hop
+            for kind in (0, 1):
+
+                @pl.when(condition)
+                def _():
+                    pltpu.make_async_remote_copy(
+                        src_ref=col.at[level, kind],
+                        dst_ref=col.at[level, kind],
+                        send_sem=f_send.at[0, 0],
+                        recv_sem=z_recv.at[level, kind],
+                        device_id=(peers[0], z),
+                        device_id_type=pl.DeviceIdType.MESH,
+                    ).wait_recv()
+
+                if hop < depth - 1:
+                    more = has_up if way == 0 else has_down
+                    along(tag, level, kind, way, jnp.logical_and(condition, more))
+            spread(tag, level, condition)
+            keep(tag, level, condition)
+            here.append((tag, level, condition))
+        for turn in turns[-2 if hop > 1 else -1 :]:
+            relay(*turn)
+        turns += here
+    for turn in turns[-2:]:
+        relay(*turn)
+    for turn in turns:
+        finish(*turn)
+        if turn[0]:
+            kept(*turn)
+    for kind in (0, 1):
+        pltpu.make_async_remote_copy(
+            src_ref=twin.at[kind],
+            dst_ref=twin.at[kind],
+            send_sem=f_send.at[0, 0],
+            recv_sem=twin_recv.at[kind],
+            device_id=(peers[4], z),
+            device_id_type=pl.DeviceIdType.MESH,
+        ).wait_recv()
+    for condition, make in started:
+
+        @pl.when(condition)
+        def _():
+            make().wait_send()
+
+
+def swap_blocks(pay):
+    devices = lax.axis_size(("dp", "tensor"))
+    depth = lax.axis_size("tensor")
+    slots = devices - 2
+    tags = 2 * depth - 1
+    block = pay.shape[1:]
+    dma = pltpu.SemaphoreType.DMA
+    return pl.pallas_call(
+        exchange,
+        out_shape=(
+            jax.ShapeDtypeStruct((slots,) + block, pay.dtype),
+            jax.ShapeDtypeStruct((2,) + block, pay.dtype),
+        ),
+        in_specs=[pl.BlockSpec(memory_space=pltpu.VMEM)],
+        out_specs=(pl.BlockSpec(memory_space=pl.ANY), pl.BlockSpec(memory_space=pl.ANY)),
+        scratch_shapes=[
+            pltpu.VMEM((depth, 2) + block, pay.dtype),
+            dma((tags, 2, 2)),
+            dma((depth, 2)),
+            dma((tags, 6)),
+            dma((tags, 3)),
+            dma((slots,)),
+            dma((2,)),
+            dma((tags,)),
+        ],
+        compiler_params=pltpu.CompilerParams(collective_id=1, has_side_effects=True),
+    )(pay)
+
+
 def gather_body(
     img_hidden, img_down, img_pooled, txt_hidden, txt_proj, log_temp, bias, match, window_index
 ):
@@ -180,34 +448,44 @@
     txt_unit, txt_len = unit_rows(txt_emb)
     image_low = img_unit.astype(jnp.bfloat16)
     text_low = txt_unit.astype(jnp.bfloat16)
-    texts = lax.all_gather(text_low, both, axis=0, tiled=True)
-    images = lax.all_gather(image_low, both, axis=0, tiled=True)
-    matches = lax.all_gather(match, both, axis=0, tiled=True)
+    matches = lax.all_gather(match, both, axis=0, tiled=True).reshape(devices, rows)
     scale = jnp.exp(log_temp[0])
     shift_value = bias[0]
-    window = window_index[0]
-    every = lax.iota(jnp.int32, devices * rows)
+    first = window_index[0] == 0
+    pay = jnp.where(first, jnp.stack([text_low, image_low]), jnp.stack([image_low, text_low]))
+    slots, twin = swap_blocks(pay)
+    count = devices // 2 - 1
+    start = jnp.where(first, pay, twin)
+    away = jnp.where(first, 0, devices // 2)
     own = position * rows + lax.iota(jnp.int32, rows)
-    nt = (((1,), (1,)), ((), ()))
-
-    logit = scale * lax.dot_general(image_low, texts, nt, preferred_element_type=jnp.float32) + shift_value
-    offset = (position - every // rows) % devices
-    inside = (offset // STEPS == window)[None, :]
-    loss, slope = stable_terms(logit, match[:, None] == every[None, :])
-    row_loss = jnp.sum(jnp.where(inside, loss, 0.0), axis=1)
-    coef = jnp.where(inside, slope * scale, 0.0).astype(jnp.bfloat16)
-    image_dunit = jnp.dot(coef, texts, preferred_element_type=jnp.float32)
-
-    logit = scale * lax.dot_general(text_low, images, nt, preferred_element_type=jnp.float32) + shift_value
-    offset = (every // rows - position) % devices
-    inside = (offset // STEPS == window)[None, :]
-    _, slope = stable_terms(logit, matches[None, :] == own[:, None])
-    coef = jnp.where(inside, slope * scale, 0.0).astype(jnp.bfloat16)
-    text_dunit = jnp.dot(coef, images, preferred_element_type=jnp.float32)
+    steps = 1 + lax.iota(jnp.int32, count)
+
+    def side(kind, left, sign, texts_here):
+        far = slots[kind * count : (kind + 1) * count].reshape(count * rows, -1)
+        near = start[kind]
+        owners = jnp.concatenate([(position + away)[None], position - sign * steps]) % devices
+        columns = (owners[:, None] * rows + lax.iota(jnp.int32, rows)[None, :]).reshape(-1)
+        wanted = jnp.where(texts_here, match, own)
+        offered = jnp.where(texts_here, columns, matches[owners].reshape(-1))
+        nt = (((1,), (1,)), ((), ()))
+
+        def part(block, offered):
+            cosine = lax.dot_general(left, block, nt, preferred_element_type=jnp.float32)
+            logit = scale * cosine + shift_value
+            loss, slope = stable_terms(logit, wanted[:, None] == offered[None, :])
+            coef = (slope * scale).astype(jnp.bfloat16)
+            return jnp.sum(loss, axis=1), jnp.dot(coef, block, preferred_element_type=jnp.float32)
+
+        near_loss, near_sum = part(near, offered[:rows])
+        far_loss, far_sum = part(far, offered[rows:])
+        return near_loss + far_loss, near_sum + far_sum
+
+    loss_a, sum_a = side(0, pay[1], 1, first)
+    loss_b, sum_b = side(1, pay[0], -1, jnp.logical_not(first))
     return (
-        tangent(image_dunit, img_unit, img_len),
-        tangent(text_dunit, txt_unit, txt_len),
-        row_loss,
+        tangent(jnp.where(first, sum_a, sum_b), img_unit, img_len),
+        tangent(jnp.where(first, sum_b, sum_a), txt_unit, txt_len),
+        jnp.where(first, loss_a, loss_b),
     )
 
 
@@ -225,5 +503,5 @@
     )
     out_specs = (P(("dp", "tensor"), None), P(("dp", "tensor"), None), P(("dp", "tensor")))
     whole = mesh.shape["dp"] * mesh.shape["tensor"]
-    body = gather_body if whole <= 2 * STEPS else ring_body
+    body = gather_body if whole == 2 * STEPS and mesh.shape["dp"] == 8 else ring_body
     return jax.shard_map(body, mesh=mesh, in_specs=in_specs, out_specs=out_specs, check_vma=False)

time: 239 us -> 232 us (0.971)
  Pallas kernels: 0 us -> 78.2 us
  blocking collectives: 147 us -> 84.9 us
  waiting for transfers between devices: 39.4 us -> 20.4 us
  between operations: 16.1 us -> 2.83 us
  matrix products: 27.9 us -> 16.6 us
  starting transfers between devices: 0.08 us -> 10.9 us
  local copies, waits for them, and re-layouts: 2.35 us -> 8.38 us
  other arithmetic: 5.55 us -> 8.96 us
    all_to_all x2 -> x0, blocking collectives: 82.2 us -> none  [scatter_sum(): got = lax.all_to_all(pieces, axis, 0, 0).astype(jnp.float32)]
    pallas_call x0 -> x1, Pallas kernels: none -> 78.2 us  [swap_blocks(): pl.pallas_call(exchange, out_shape=(jax.ShapeDtypeStruct((slots,) + block...]
    all_gather x2 -> x0, waiting for transfers between devices: 39.4 us -> none  [the longest x1 39.3 us: gather_body(): texts = lax.all_gather(text_low, both, axis=0, tiled=True)]
    all_to_all x0 -> x2, waiting for transfers between devices: none -> 20.4 us  [scatter_sum(): got = lax.all_to_all(pieces, axis, 0, 0).astype(jnp.float32)]
    all_gather x1, blocking collectives: 64.8 us -> 84.9 us  [gather_body(): lax.all_gather(match, both, axis=0, tiled=True).reshape(devices, rows)]
    dot_general x3 -> x8, matrix products: 22.7 us -> 9.49 us  [the longest x4 4.8 us: part(): lax.dot_general(left, block, nt, preferred_element_type=jnp.float32)]
    all_to_all x0 -> x2, starting transfers between devices: none -> 10.9 us  [scatter_sum(): got = lax.all_to_all(pieces, axis, 0, 0).astype(jnp.float32)]
    slice x0 -> x5, local copies, waits for them, and re-layouts: none -> 4.15 us  [the longest x1 4.14 us: side(): far = slots[kind * count:(kind + 1) * count].reshape(count * rows, -1)]
  transfers between devices with their start and end apart: 2 -> 2, of which waited for: 1 -> 1; matrix products, arithmetic and copies ran while one was open for 7% -> 3% of each run, Pallas kernels for 0% -> 0%
where the time goes in v2:
time: 232 us; the launch traced here: 231 us
  blocking collectives  84.9 us (37%)
  Pallas kernels  78.2 us (34%)
  waiting for transfers between devices  20.4 us (9%)
  matrix products  16.6 us (7%)
  starting transfers between devices  10.9 us (5%)
  other arithmetic  8.96 us (4%)
  local copies, waits for them, and re-layouts  8.38 us (4%)
  between operations  2.83 us (1%)
    all_gather x1, blocking collectives, gather_body(): lax.all_gather(match, both, axis=0, tiled=True).reshape(devices, rows)  84.9 us
    pallas_call x1, Pallas kernels, swap_blocks(): pl.pallas_call(exchange, out_shape=(jax.ShapeDtypeStruct((slots,) + block...  78.2 us
    all_to_all x2, waiting for transfers between devices, scatter_sum(): got = lax.all_to_all(pieces, axis, 0, 0).astype(jnp.float32)  20.4 us
    all_to_all x2, starting transfers between devices, scatter_sum(): got = lax.all_to_all(pieces, axis, 0, 0).astype(jnp.float32)  10.9 us
    dot_general x4, matrix products, part(): lax.dot_general(left, block, nt, preferred_element_type=jnp.float32)  4.8 us
    dot_general x4, matrix products, part(): jnp.dot(coef, block, preferred_element_type=jnp.float32)  4.7 us
  transfers between devices with their start and end apart: 2, of which 1 were waited for; matrix products, arithmetic and copies ran while one was open for 3% of the time, Pallas kernels for 0%

profile of v2, /device:TPU:0, one launch (start us, length us, event | category | flops | bytes accessed | tf_op | source)
XLA Modules:
  0.0 231.2 jit_solution(10114212178739413873)
XLA Ops:
  0.6 0.0 copy-start
  0.6 0.0 copy-start.9
  0.7 1.7 copy-done
  2.3 4.1 %convolution_convert_fusion = bf16[512,1152]{1,0:T(8,128)(2,1)} fusion(bf16[512,1076]{0,1:T(8,128)(2,1)} %param.9, bf16[1076,1152]{1,0:T(8,128)(2,1)S(1)} %copy-done), kind=kOutput, calls=%fused_computation.2 | convolution fusion | flops 1269891072 | bytes 4760576 | tf_op jit(solution)/shard_map/dot_general | solution.py:445
  6.5 0.0 copy-start.10
  6.5 6.5 %all-to-all-start.1 = ((bf16[4,128,1152]{2,1,0:T(8,128)(2,1)}), bf16[4,128,1152]{2,1,0:T(8,128)(2,1)}, u32[]{:S(2)}, u32[]{:S(2)}) async-start(bf16[4,128,1152]{2,1,0:T(8,128)(2,1)} %bitcast.87), calls=%async_computation.1 | async-start | bytes 2359296 | tf_op jit(solution)/shard_map/all_to_all | solution.py:153
  13.6 0.0 copy-done.9
  13.6 84.9 %all-gather = s32[32,1,128]{2,1,0:T(1,128)S(1)} all-gather(s32[1,1,128]{2,1,0:T(1,128)S(1)} %bitcast.89), channel_id=1, replica_groups=mesh['dp'=8,'tensor'=4] {'dp','tensor'}, dimensions={0}, use_global_device_ids=true | all-gather | bytes 16896 | tf_op jit(solution)/shard_map/all_gather | solution.py:451
  98.5 0.1 fusion.47
  98.6 0.6 gather_fusion.1
  99.2 0.1 fusion.46
  99.3 0.6 gather_fusion
  99.9 0.1 fusion.41
  99.9 0.1 fusion.40
  100.0 0.1 add_select_fusion.1
  100.1 0.1 add_select_fusion
  100.2 0.0 copy-done.10
  100.2 3.0 %convolution_convert_fusion.1 = bf16[512,1152]{1,0:T(8,128)(2,1)} fusion(bf16[512,288]{0,1:T(8,128)(2,1)S(1)} %copy-done.10, bf16[288,1152]{1,0:T(8,128)(2,1)} %param.13), kind=kOutput, calls=%fused_computation.3 | convolution fusion | flops 340328448 | bytes 2138112 | tf_op jit(solution)/shard_map/dot_general | solution.py:443
  103.2 0.0 copy-start.3
  103.2 0.0 all-to-all-done.1
  103.2 4.4 %all-to-all-start = ((bf16[4,128,1152]{2,1,0:T(8,128)(2,1)}), bf16[4,128,1152]{2,1,0:T(8,128)(2,1)}, u32[]{:S(2)}, u32[]{:S(2)}) async-start(bf16[4,128,1152]{2,1,0:T(8,128)(2,1)} %bitcast.88), calls=%async_computation | async-start | bytes 2359296 | tf_op jit(solution)/shard_map/all_to_all | solution.py:153
  109.0 1.5 convert_reduce_fusion
  110.5 0.0 copy-done.3
  110.5 0.2 multiply_reduce_fusion.2
  110.7 0.8 convert_bitcast_fusion
  111.5 20.4 %all-to-all-done = bf16[4,128,1152]{2,1,0:T(8,128)(2,1)} async-done(((bf16[4,128,1152]{2,1,0:T(8,128)(2,1)}), bf16[4,128,1152]{2,1,0:T(8,128)(2,1)}, u32[]{:S(2)}, u32[]{:S(2)}) %all-to-all-start) | async-done | bytes 1179680 | tf_op jit(solution)/shard_map/all_to_all | solution.py:153
  131.9 0.0 copy-start.5
  131.9 1.5 convert_reduce_fusion.1
  133.4 0.0 copy-start.1
  133.5 0.1 multiply_reduce_fusion.3
  133.6 0.7 copy-done.1
  134.3 0.1 fusion.8
  134.4 0.0 copy-start.4
  134.4 0.7 copy-done.4
  135.1 0.0 copy-done.5
  135.1 0.9 maximum_select_fusion.pay
  136.0 78.2 %shard_map.112 = (bf16[30,128,1152]{2,1,0:T(8,128)(2,1)}, bf16[2,128,1152]{2,1,0:T(8,128)(2,1)}) custom-call(bf16[2,128,1152]{2,1,0:T(8,128)(2,1)} %maximum_select_fusion.pay), custom_call_target="tpu_custom_call" | custom-call | tf_op jit(solution)/shard_map/pallas_call | solution.py:413
  214.2 0.0 copy-start.6
  214.2 1.4 broadcast_select_fusion
  215.7 1.3 add_reduce_fusion.2
  216.9 1.2 fusion.23
  218.2 0.0 copy-done.6
  218.2 0.3 add_reduce_fusion.3
  218.5 1.1 fusion.22
  219.6 4.1 %fusion.59 = (bf16[15,128,1152]{2,1,0:T(8,128)(2,1)S(1)}, bf16[15,128,1152]{2,1,0:T(8,128)(2,1)S(1)}) fusion(bf16[30,128,1152]{2,1,0:T(8,128)(2,1)} %get-tuple-element.6), kind=kLoop, calls=%fused_computation.131 | loop fusion | bytes 17694720 | tf_op jit(solution)/shard_map/slice | solution.py:464
  223.8 0.0 copy-start.8
  223.8 1.6 add_reduce_fusion.1
  225.4 0.0 copy-done.8
  225.4 1.1 convolution_add_fusion.1
  226.5 0.0 copy-start.2
  226.5 0.0 copy-start.7
  226.5 1.6 add_reduce_fusion
  228.1 0.0 copy-done.2
  228.1 0.0 copy-done.7
  228.2 1.2 multiply_reduce_fusion
  229.4 1.3 subtract_divide_fusion
  230.7 0.5 broadcast_select_fusion.4
  (11 shorter events, 0.1 us)
Async XLA Ops:
  0.6 1.7 copy-start
  0.6 13.0 %copy-start.9 = (s32[128]{0:T(128)S(1)}, s32[128]{0:T(128)}, u32[]{:S(2)}) copy-start(s32[128]{0:T(128)} %param.16) | copy-start | bytes 1540
  6.5 93.7 %copy-start.10 = (bf16[512,288]{0,1:T(8,128)(2,1)S(1)}, bf16[512,288]{0,1:T(8,128)(2,1)}, u32[]{:S(2)}) copy-start(bf16[512,288]{0,1:T(8,128)(2,1)} %param.12) | copy-start | bytes 884740
  6.5 96.7 %all-to-all-start.1 = ((bf16[4,128,1152]{2,1,0:T(8,128)(2,1)}), bf16[4,128,1152]{2,1,0:T(8,128)(2,1)}, u32[]{:S(2)}, u32[]{:S(2)}) async-start(bf16[4,128,1152]{2,1,0:T(8,128)(2,1)} %bitcast.87), calls=%async_computation.1 | async-start | bytes 2359296 | tf_op jit(solution)/shard_map/all_to_all | solution.py:153
  103.2 7.3 %copy-start.3 = (bf16[128,1152]{1,0:T(8,128)(2,1)S(1)}, bf16[128,1152]{1,0:T(8,128)(2,1)}, u32[]{:S(2)}) copy-start(bf16[128,1152]{1,0:T(8,128)(2,1)} %param.11) | copy-start | bytes 884740
  103.2 28.7 %all-to-all-start = ((bf16[4,128,1152]{2,1,0:T(8,128)(2,1)}), bf16[4,128,1152]{2,1,0:T(8,128)(2,1)}, u32[]{:S(2)}, u32[]{:S(2)}) async-start(bf16[4,128,1152]{2,1,0:T(8,128)(2,1)} %bitcast.88), calls=%async_computation | async-start | bytes 2359296 | tf_op jit(solution)/shard_map/all_to_all | solution.py:153
  131.9 3.2 %copy-start.5 = (bf16[1,128,1152]{2,1,0:T(8,128)(2,1)S(1)}, bf16[1,128,1152]{2,1,0:T(8,128)(2,1)}, u32[]{:S(2)}) copy-start(bf16[1,128,1152]{2,1,0:T(8,128)(2,1)} %convert_bitcast_fusion) | copy-start | bytes 884740
  133.4 0.8 copy-start.1
  134.4 0.7 copy-start.4
  214.2 3.9 %copy-start.6 = (bf16[2,128,1152]{2,1,0:T(8,128)(2,1)S(1)}, bf16[2,128,1152]{2,1,0:T(8,128)(2,1)}, u32[]{:S(2)}) copy-start(bf16[2,128,1152]{2,1,0:T(8,128)(2,1)} %maximum_select_fusion.pay) | copy-start | bytes 1769476
  223.8 1.6 copy-start.8
  226.5 1.6 copy-start.2
  226.5 1.6 copy-start.7
